TPU v7x, 32 devices: a whole 2x2x4 slice. The times are simulated.
32 devices in a mesh: patch: 32 (over z, y, x, core).
Axes of the slice: x: 2, y: 2, z: 4, core: 2. Of those that a mesh axis runs over, the one named last changes fastest.
Arguments:
- positions: float32 [3, 65536], P(None, 'patch'), may hold values from -6 to 6
- densities: float32 [3, 65536], P(None, 'patch'), may hold values from -6 to 6
- near_src: int32 [512, 8], P('patch'), may hold values from 0 to 511, as said below
- near_count: int32 [512], P('patch'), may hold values from 1 to 8
- far_slot: int32 [512, 32], P('patch'), may hold values from 0 to 127
- far_class: int32 [512, 32], P('patch'), may hold values from 0 to 188
- far_count: int32 [512], P('patch'), may hold values from 1 to 32
- requests: int32 [32, 32, 4], P('patch'), may hold values from 0 to 15, as said below
- up_basis: bfloat16 [512, 144, 384], P('patch'), may hold values from -0.3125 to 0.3125
- transfer_table: bfloat16 [189, 20736], replicated, may hold values from -0.5 to 0.5
- down_basis: bfloat16 [512, 144, 9, 128], P('patch'), may hold values from -0.09375 to 0.09375
Outputs:
- shape_grad: float32 [3, 65536], P(None, 'patch')
Inputs may be any that keep to these rules, and one draw needn't show every extreme that they name: `near_src`: the source leaf of each near-field block is held by the device of its target leaf or by the device just before or after it along patch. `requests`: each row names 4 different leaves of the source device, by their index on that device.
All inputs are finite; a program needn't handle non-finite values.
Results may differ from a plain program's by a relative error of at most 0.0042.
Values may be sent and summed in bfloat16 or wider, within the bound.
A program may use at most 192 MiB of HBM per device.

v0:
```python
import math

import jax
import jax.numpy as jnp
from jax import lax
from jax.sharding import PartitionSpec as P

KERNEL = 1.0 / (8.0 * math.pi)
BLOB = 0.25


def with_halo(x, sides, width):
    for axis, dim in sides:
        peers, length = (lax.axis_size(axis), x.shape[dim])
        up = [(i, (i + 1) % peers) for i in range(peers - 1)]
        down = [(j, i) for i, j in up]
        last = lax.slice_in_dim(x, length - width, length, axis=dim)
        first = lax.slice_in_dim(x, 0, width, axis=dim)
        before = lax.ppermute(last, axis, up)
        after = lax.ppermute(first, axis, down)
        x = jnp.concatenate([before, x, after], axis=dim)
    return x


def passed_along(x, axis, by):
    peers = lax.axis_size(axis)
    pairs = [(i, i + by) for i in range(peers) if 0 <= i + by < peers]
    return lax.ppermute(x, axis, pairs)


def pair_terms(target, source):
    xt = target[:, :3]
    ft = target[:, 3:]
    xs = source[:, :3]
    fs = source[:, 3:]
    sep = xt[:, :, :, None] - xs[:, :, None, :]
    rho_sq = jnp.sum(sep * sep, axis=1) + BLOB
    inv_one = lax.rsqrt(rho_sq)
    inv_three = inv_one / rho_sq
    inv_five = inv_three / rho_sq
    fa = ft[:, :, :, None]
    fb = fs[:, :, None, :]
    prod_ab = jnp.sum(fa * fb, axis=1)
    prod_ar = jnp.sum(fa * sep, axis=1)
    prod_br = jnp.sum(fb * sep, axis=1)
    first = (fa * prod_br[:, None] + fb * prod_ar[:, None] - prod_ab[:, None] * sep) * inv_three[
        :, None
    ]
    second = 3.0 * (prod_ar * prod_br * inv_five)[:, None] * sep
    return (first - second) * KERNEL


def one_hot(indices, count, dtype):
    return (indices[:, None] == jnp.arange(count, dtype=jnp.int32)[None, :]).astype(dtype)


def select_rows(indices, data):
    flat = data.reshape(data.shape[0], -1)
    picked = jnp.dot(
        one_hot(indices, data.shape[0], jnp.float32), flat, precision=lax.Precision.HIGHEST
    )
    return picked.reshape((indices.shape[0],) + data.shape[1:])


def add_rows(total, indices, values):
    hot = one_hot(indices, total.shape[0], jnp.float32)
    flat = values.reshape(values.shape[0], -1)
    added = jnp.dot(hot.T, flat, precision=lax.Precision.HIGHEST)
    return total + added.reshape(total.shape)


def per_device(
    positions,
    densities,
    near_src,
    near_count,
    far_slot,
    far_class,
    far_count,
    requests,
    up_basis,
    transfer_table,
    down_basis,
):
    leaf_num = near_count.shape[0]
    per_leaf = positions.shape[1] // leaf_num
    width = up_basis.shape[1]
    slot_num = near_src.shape[1]
    far_num = far_slot.shape[1]
    device = lax.axis_index("patch")
    stacked = jnp.concatenate([positions, densities], 0)
    window = with_halo(stacked, (("patch", 1),), stacked.shape[1])
    window = window.reshape(6, 3 * leaf_num, per_leaf).transpose(1, 0, 2)
    local = stacked.reshape(6, leaf_num, per_leaf).transpose(1, 0, 2)
    offset = (device - 1) * leaf_num
    start_state = (
        jnp.zeros((leaf_num, 3, per_leaf), jnp.float32),
        jnp.zeros((3 * leaf_num, 3, per_leaf), jnp.float32),
    )

    def near_step(slot, carry):
        tgt_sum, src_part = carry
        index = near_src[:, slot] - offset
        live = (slot < near_count).astype(jnp.float32)
        terms = pair_terms(local, select_rows(index, window)) * live[:, None, None, None]
        tgt_sum = tgt_sum + jnp.sum(terms, axis=3)
        src_part = add_rows(src_part, index, -jnp.sum(terms, axis=2))
        return (tgt_sum, src_part)

    tgt_sum, src_part = lax.fori_loop(0, slot_num, near_step, start_state)
    near = tgt_sum + src_part[leaf_num : 2 * leaf_num]
    for step_by, piece in ((-1, src_part[:leaf_num]), (1, src_part[2 * leaf_num :])):
        near = near + passed_along(piece, "patch", step_by)
    dens_leaf = local[:, 3:]
    dens_round = dens_leaf.reshape(leaf_num, 3 * per_leaf).astype(jnp.bfloat16)
    moments = jnp.einsum(
        "lrq,lq->lr", up_basis, dens_round, preferred_element_type=jnp.float32
    ).astype(jnp.bfloat16)
    asked = lax.all_to_all(requests[0], "patch", split_axis=0, concat_axis=0, tiled=True)
    replies = moments[asked].reshape(asked.shape[0], asked.shape[1] * width)
    table = lax.all_to_all(replies, "patch", split_axis=0, concat_axis=0, tiled=True).reshape(
        -1, width
    )
    operators = jnp.take(transfer_table, far_class.reshape(-1), axis=0).reshape(
        leaf_num, far_num, width, width
    )
    live_far = (jnp.arange(far_num, dtype=jnp.int32)[None, :] < far_count[:, None]).astype(
        jnp.bfloat16
    )
    sources = (
        jnp.take(table, far_slot.reshape(-1), axis=0).reshape(leaf_num, far_num, width)
        * live_far[:, :, None]
    )
    expansion = jnp.einsum("lsij,lsj->li", operators, sources, preferred_element_type=jnp.float32)
    expansion = expansion.astype(jnp.bfloat16)
    field = jnp.einsum("lr,lrqp->lqp", expansion, down_basis, preferred_element_type=jnp.float32)
    far = jnp.einsum(
        "lcp,lckp->lkp",
        dens_leaf,
        field.reshape(leaf_num, 3, 3, per_leaf),
        precision=lax.Precision.HIGHEST,
    )
    return (near + far).transpose(1, 0, 2).reshape(3, leaf_num * per_leaf)


def solution(mesh):
    placed = (
        P(None, "patch"),
        P(None, "patch"),
        P("patch", None),
        P("patch"),
        P("patch", None),
        P("patch", None),
        P("patch"),
        P("patch", None, None),
        P("patch", None, None),
        P(),
        P("patch", None, None, None),
    )
    return jax.shard_map(
        per_device, mesh=mesh, in_specs=placed, out_specs=P(None, "patch"), check_vma=False
    )
```

profile of v0, /device:TPU:3, one launch (start us, length us, event | category | flops | bytes accessed | tf_op | source)
XLA Modules:
  0.0 220.4 jit_solution(13064873262900393364)
XLA Ops:
  0.0 0.9 pad_maximum_fusion
  0.9 2.6 %collective-permute-start.1 = (f32[6,2048]{1,0:T(8,128)S(1)}, f32[6,2048]{1,0:T(8,128)S(1)}, u32[]{:S(2)}, u32[]{:S(2)}) collective-permute-start(f32[6,2048]{1,0:T(8,128)S(1)} %get-tuple-element.204), channel_id=1, source_target_pairs={{1,0},{2,1},{3,2},{4,3},{5,4},{6,5},{7,6},{8,7},{9,8},{10,9},{11,1... | collective-permute-start | bytes 147464 | tf_op jit(solution)/shard_map/ppermute | solution.py:20
  3.5 3.9 %collective-permute-start = (f32[6,2048]{1,0:T(8,128)S(1)}, f32[6,2048]{1,0:T(8,128)S(1)}, u32[]{:S(2)}, u32[]{:S(2)}) collective-permute-start(f32[6,2048]{1,0:T(8,128)S(1)} %get-tuple-element.204), channel_id=1, source_target_pairs={{0,1},{1,2},{2,3},{3,4},{4,5},{5,6},{6,7},{7,8},{8,9},{9,10},{10,1... | collective-permute-start | bytes 147464 | tf_op jit(solution)/shard_map/ppermute | solution.py:19
  7.4 1.4 copy.36
  8.8 5.7 %all-to-all-start = ((s32[32,1,4]{2,1,0:T(1,128)}), s32[32,1,4]{2,1,0:T(1,128)S(1)}, u32[]{:S(2)}, u32[]{:S(2)}) async-start(s32[32,1,4]{2,1,0:T(1,128)} %copy.36), calls=%async_computation | async-start | bytes 32768 | tf_op jit(solution)/shard_map/all_to_all | solution.py:119
  14.5 0.8 reshape.227
  15.3 0.7 compare_and_fusion.1
  16.1 0.8 reshape.229
  16.9 0.8 fusion.32
  17.7 0.7 fusion.38
  18.4 40.6 %gather_fusion = bf16[512,20736]{1,0:T(8,128)(2,1)} fusion(bf16[189,20736]{1,0:T(8,128)(2,1)} %param.22, s32[1024]{0:T(1024)S(1)} %pad_clamp_fusion.2), kind=kCustom, calls=%fused_computation | custom fusion | bytes 42469376 | tf_op jit(solution)/shard_map/jit(_take)/gather | solution.py:124
  59.0 67.3 %gather.16 = bf16[16,32,144,144]{3,2,1,0:T(8,128)(2,1)} reshape(bf16[512,20736]{1,0:T(8,128)(2,1)} %gather_fusion) | data formatting | bytes 42467328 | tf_op jit(solution)/shard_map/jit(_take)/gather | solution.py:124
  126.6 0.8 gather_fusion.1
  127.6 0.5 broadcast.181
  128.2 0.9 reduce.3
  129.0 0.7 reshape.271
  129.8 5.8 %all-to-all-start.1 = ((bf16[32,2,288]{2,1,0:T(2,128)(2,1)}), bf16[32,2,288]{2,1,0:T(2,128)(2,1)S(1)}, u32[]{:S(2)}, u32[]{:S(2)}) async-start(bf16[32,2,288]{2,1,0:T(2,128)(2,1)} %reshape.271), calls=%async_computation.1 | async-start | bytes 98304 | tf_op jit(solution)/shard_map/all_to_all | solution.py:121
  135.7 56.9 %while.16 = (s32[]{:T(128)}, f32[16,3,128]{2,1,0:T(4,128)S(1)}, f32[48,3,128]{2,0,1:T(8,128)S(1)}, f32[16,6,128]{2,1,0:T(8,128)S(1)}, s32[16,8]{0,1:T(8,128)}, /...) while((s32[]{:T(128)}, f32[16,3,128]{2,1,0:T(4,128)S(1)}, ...), condition=%wide.region_7.0_spmd.clone, body=%wide.region_0.0_spmd.clone.sunk | while | flops 27962928 | bytes 15712836 | solution.py:110
  135.7 0.7 subtract_bitcast_fusion.2
  136.7 2.2 %fusion.58 = (f32[16,128,128]{2,1,0:T(8,128)S(1)}, f32[16,128,128]{2,1,0:T(8,128)S(1)}, f32[16,128,128]{2,1,0:T(8,128)S(1)}, f32[16,128,128]{2,1,0:T(8,128)S(1)}) fusion(f32[16,3,128]{2,1,0:T(4,128)S(1)} %copy.104, f32[16,3,128]{2,1,0:T(4,128)S(1)} %get-tuple-element.270, f32[16,3,128]{2,1,0:T(4,128)S(1)} %get-tuple-element.271, ...), kind=kLoop, calls=%fused_computation.14.clone.1 | loop fusion | flops 6029312 | bytes 4292608 | tf_op jit(solution)/shard_map/while/body/eval_jaxpr/reduce_sum | solution.py:37
  139.4 3.0 %fusion.59 = (f32[16,3,128]{2,1,0:T(4,128)S(1)}, f32[16,3,128]{2,1,0:T(4,128)S(1)}) fusion(f32[16]{0:T(128)S(1)} %compare_select_fusion.7, f32[16,128,128]{2,1,0:T(8,128)S(1)} %get-tuple-element.276, f32[16,128,128]{2,1,0:T(8,128)S(1)} %get-tuple-element.277, f32[16,128,128]{2,1,0:T(8,128)S(1)} %get-tuple-element.278, ...), kind=kLoop, calls=%fused_computation.16.clone.1 | loop fusion | flops 9424896 | bytes 5390400 | tf_op jit(solution)/shard_map/while/body/eval_jaxpr/reduce_sum | solution.py:107
  142.8 0.7 subtract_bitcast_fusion.2
  143.8 2.2 %fusion.58 = (f32[16,128,128]{2,1,0:T(8,128)S(1)}, f32[16,128,128]{2,1,0:T(8,128)S(1)}, f32[16,128,128]{2,1,0:T(8,128)S(1)}, f32[16,128,128]{2,1,0:T(8,128)S(1)}) fusion(f32[16,3,128]{2,1,0:T(4,128)S(1)} %copy.104, f32[16,3,128]{2,1,0:T(4,128)S(1)} %get-tuple-element.270, f32[16,3,128]{2,1,0:T(4,128)S(1)} %get-tuple-element.271, ...), kind=kLoop, calls=%fused_computation.14.clone.1 | loop fusion | flops 6029312 | bytes 4292608 | tf_op jit(solution)/shard_map/while/body/eval_jaxpr/reduce_sum | solution.py:37
  146.5 3.0 %fusion.59 = (f32[16,3,128]{2,1,0:T(4,128)S(1)}, f32[16,3,128]{2,1,0:T(4,128)S(1)}) fusion(f32[16]{0:T(128)S(1)} %compare_select_fusion.7, f32[16,128,128]{2,1,0:T(8,128)S(1)} %get-tuple-element.276, f32[16,128,128]{2,1,0:T(8,128)S(1)} %get-tuple-element.277, f32[16,128,128]{2,1,0:T(8,128)S(1)} %get-tuple-element.278, ...), kind=kLoop, calls=%fused_computation.16.clone.1 | loop fusion | flops 9424896 | bytes 5390400 | tf_op jit(solution)/shard_map/while/body/eval_jaxpr/reduce_sum | solution.py:107
  149.9 0.7 subtract_bitcast_fusion.2
  150.9 2.2 %fusion.58 = (f32[16,128,128]{2,1,0:T(8,128)S(1)}, f32[16,128,128]{2,1,0:T(8,128)S(1)}, f32[16,128,128]{2,1,0:T(8,128)S(1)}, f32[16,128,128]{2,1,0:T(8,128)S(1)}) fusion(f32[16,3,128]{2,1,0:T(4,128)S(1)} %copy.104, f32[16,3,128]{2,1,0:T(4,128)S(1)} %get-tuple-element.270, f32[16,3,128]{2,1,0:T(4,128)S(1)} %get-tuple-element.271, ...), kind=kLoop, calls=%fused_computation.14.clone.1 | loop fusion | flops 6029312 | bytes 4292608 | tf_op jit(solution)/shard_map/while/body/eval_jaxpr/reduce_sum | solution.py:37
  153.6 3.0 %fusion.59 = (f32[16,3,128]{2,1,0:T(4,128)S(1)}, f32[16,3,128]{2,1,0:T(4,128)S(1)}) fusion(f32[16]{0:T(128)S(1)} %compare_select_fusion.7, f32[16,128,128]{2,1,0:T(8,128)S(1)} %get-tuple-element.276, f32[16,128,128]{2,1,0:T(8,128)S(1)} %get-tuple-element.277, f32[16,128,128]{2,1,0:T(8,128)S(1)} %get-tuple-element.278, ...), kind=kLoop, calls=%fused_computation.16.clone.1 | loop fusion | flops 9424896 | bytes 5390400 | tf_op jit(solution)/shard_map/while/body/eval_jaxpr/reduce_sum | solution.py:107
  157.1 0.7 subtract_bitcast_fusion.2
  158.1 2.2 %fusion.58 = (f32[16,128,128]{2,1,0:T(8,128)S(1)}, f32[16,128,128]{2,1,0:T(8,128)S(1)}, f32[16,128,128]{2,1,0:T(8,128)S(1)}, f32[16,128,128]{2,1,0:T(8,128)S(1)}) fusion(f32[16,3,128]{2,1,0:T(4,128)S(1)} %copy.104, f32[16,3,128]{2,1,0:T(4,128)S(1)} %get-tuple-element.270, f32[16,3,128]{2,1,0:T(4,128)S(1)} %get-tuple-element.271, ...), kind=kLoop, calls=%fused_computation.14.clone.1 | loop fusion | flops 6029312 | bytes 4292608 | tf_op jit(solution)/shard_map/while/body/eval_jaxpr/reduce_sum | solution.py:37
  160.7 3.0 %fusion.59 = (f32[16,3,128]{2,1,0:T(4,128)S(1)}, f32[16,3,128]{2,1,0:T(4,128)S(1)}) fusion(f32[16]{0:T(128)S(1)} %compare_select_fusion.7, f32[16,128,128]{2,1,0:T(8,128)S(1)} %get-tuple-element.276, f32[16,128,128]{2,1,0:T(8,128)S(1)} %get-tuple-element.277, f32[16,128,128]{2,1,0:T(8,128)S(1)} %get-tuple-element.278, ...), kind=kLoop, calls=%fused_computation.16.clone.1 | loop fusion | flops 9424896 | bytes 5390400 | tf_op jit(solution)/shard_map/while/body/eval_jaxpr/reduce_sum | solution.py:107
  164.2 0.7 subtract_bitcast_fusion.2
  165.2 2.2 %fusion.58 = (f32[16,128,128]{2,1,0:T(8,128)S(1)}, f32[16,128,128]{2,1,0:T(8,128)S(1)}, f32[16,128,128]{2,1,0:T(8,128)S(1)}, f32[16,128,128]{2,1,0:T(8,128)S(1)}) fusion(f32[16,3,128]{2,1,0:T(4,128)S(1)} %copy.104, f32[16,3,128]{2,1,0:T(4,128)S(1)} %get-tuple-element.270, f32[16,3,128]{2,1,0:T(4,128)S(1)} %get-tuple-element.271, ...), kind=kLoop, calls=%fused_computation.14.clone.1 | loop fusion | flops 6029312 | bytes 4292608 | tf_op jit(solution)/shard_map/while/body/eval_jaxpr/reduce_sum | solution.py:37
  167.9 3.0 %fusion.59 = (f32[16,3,128]{2,1,0:T(4,128)S(1)}, f32[16,3,128]{2,1,0:T(4,128)S(1)}) fusion(f32[16]{0:T(128)S(1)} %compare_select_fusion.7, f32[16,128,128]{2,1,0:T(8,128)S(1)} %get-tuple-element.276, f32[16,128,128]{2,1,0:T(8,128)S(1)} %get-tuple-element.277, f32[16,128,128]{2,1,0:T(8,128)S(1)} %get-tuple-element.278, ...), kind=kLoop, calls=%fused_computation.16.clone.1 | loop fusion | flops 9424896 | bytes 5390400 | tf_op jit(solution)/shard_map/while/body/eval_jaxpr/reduce_sum | solution.py:107
  171.3 0.7 subtract_bitcast_fusion.2
  172.3 2.2 %fusion.58 = (f32[16,128,128]{2,1,0:T(8,128)S(1)}, f32[16,128,128]{2,1,0:T(8,128)S(1)}, f32[16,128,128]{2,1,0:T(8,128)S(1)}, f32[16,128,128]{2,1,0:T(8,128)S(1)}) fusion(f32[16,3,128]{2,1,0:T(4,128)S(1)} %copy.104, f32[16,3,128]{2,1,0:T(4,128)S(1)} %get-tuple-element.270, f32[16,3,128]{2,1,0:T(4,128)S(1)} %get-tuple-element.271, ...), kind=kLoop, calls=%fused_computation.14.clone.1 | loop fusion | flops 6029312 | bytes 4292608 | tf_op jit(solution)/shard_map/while/body/eval_jaxpr/reduce_sum | solution.py:37
  175.0 3.0 %fusion.59 = (f32[16,3,128]{2,1,0:T(4,128)S(1)}, f32[16,3,128]{2,1,0:T(4,128)S(1)}) fusion(f32[16]{0:T(128)S(1)} %compare_select_fusion.7, f32[16,128,128]{2,1,0:T(8,128)S(1)} %get-tuple-element.276, f32[16,128,128]{2,1,0:T(8,128)S(1)} %get-tuple-element.277, f32[16,128,128]{2,1,0:T(8,128)S(1)} %get-tuple-element.278, ...), kind=kLoop, calls=%fused_computation.16.clone.1 | loop fusion | flops 9424896 | bytes 5390400 | tf_op jit(solution)/shard_map/while/body/eval_jaxpr/reduce_sum | solution.py:107
  178.4 0.7 subtract_bitcast_fusion.2
  179.4 2.2 %fusion.58 = (f32[16,128,128]{2,1,0:T(8,128)S(1)}, f32[16,128,128]{2,1,0:T(8,128)S(1)}, f32[16,128,128]{2,1,0:T(8,128)S(1)}, f32[16,128,128]{2,1,0:T(8,128)S(1)}) fusion(f32[16,3,128]{2,1,0:T(4,128)S(1)} %copy.104, f32[16,3,128]{2,1,0:T(4,128)S(1)} %get-tuple-element.270, f32[16,3,128]{2,1,0:T(4,128)S(1)} %get-tuple-element.271, ...), kind=kLoop, calls=%fused_computation.14.clone.1 | loop fusion | flops 6029312 | bytes 4292608 | tf_op jit(solution)/shard_map/while/body/eval_jaxpr/reduce_sum | solution.py:37
  182.1 3.0 %fusion.59 = (f32[16,3,128]{2,1,0:T(4,128)S(1)}, f32[16,3,128]{2,1,0:T(4,128)S(1)}) fusion(f32[16]{0:T(128)S(1)} %compare_select_fusion.7, f32[16,128,128]{2,1,0:T(8,128)S(1)} %get-tuple-element.276, f32[16,128,128]{2,1,0:T(8,128)S(1)} %get-tuple-element.277, f32[16,128,128]{2,1,0:T(8,128)S(1)} %get-tuple-element.278, ...), kind=kLoop, calls=%fused_computation.16.clone.1 | loop fusion | flops 9424896 | bytes 5390400 | tf_op jit(solution)/shard_map/while/body/eval_jaxpr/reduce_sum | solution.py:107
  185.5 0.7 subtract_bitcast_fusion.2
  186.5 2.2 %fusion.58 = (f32[16,128,128]{2,1,0:T(8,128)S(1)}, f32[16,128,128]{2,1,0:T(8,128)S(1)}, f32[16,128,128]{2,1,0:T(8,128)S(1)}, f32[16,128,128]{2,1,0:T(8,128)S(1)}) fusion(f32[16,3,128]{2,1,0:T(4,128)S(1)} %copy.104, f32[16,3,128]{2,1,0:T(4,128)S(1)} %get-tuple-element.270, f32[16,3,128]{2,1,0:T(4,128)S(1)} %get-tuple-element.271, ...), kind=kLoop, calls=%fused_computation.14.clone.1 | loop fusion | flops 6029312 | bytes 4292608 | tf_op jit(solution)/shard_map/while/body/eval_jaxpr/reduce_sum | solution.py:37
  189.2 3.0 %fusion.59 = (f32[16,3,128]{2,1,0:T(4,128)S(1)}, f32[16,3,128]{2,1,0:T(4,128)S(1)}) fusion(f32[16]{0:T(128)S(1)} %compare_select_fusion.7, f32[16,128,128]{2,1,0:T(8,128)S(1)} %get-tuple-element.276, f32[16,128,128]{2,1,0:T(8,128)S(1)} %get-tuple-element.277, f32[16,128,128]{2,1,0:T(8,128)S(1)} %get-tuple-element.278, ...), kind=kLoop, calls=%fused_computation.16.clone.1 | loop fusion | flops 9424896 | bytes 5390400 | tf_op jit(solution)/shard_map/while/body/eval_jaxpr/reduce_sum | solution.py:107
  192.6 3.4 %collective-permute-start.3 = (f32[16,3,128]{2,0,1:T(8,128)S(1)}, f32[16,3,128]{2,0,1:T(8,128)S(1)}, u32[]{:S(2)}, u32[]{:S(2)}) collective-permute-start(f32[16,3,128]{2,0,1:T(8,128)S(1)} %get-tuple-element.203), channel_id=1, source_target_pairs={{0,1},{1,2},{2,3},{3,4},{4,5},{5,6},{6,7},{7,8},{8,9},{9,10},{10,1... | collective-permute-start | bytes 73736 | tf_op jit(solution)/shard_map/ppermute | solution.py:28
  196.0 1.9 collective-permute-start.2
  198.4 2.0 gather_fusion.2
  200.6 15.7 %fusion.21 = bf16[16,1,144,1]{2,1,3,0:T(2,128)(2,1)S(1)} fusion(bf16[16,32,144,144]{3,2,1,0:T(8,128)(2,1)} %gather.16, pred[16,32]{1,0:T(8,128)(4,1)S(1)} %compare_and_fusion.1, bf16[16,32,144,1]{2,1,0,3:T(8,128)(2,1)S(1)} %multiply_bitcast_fusion), kind=kOutput, calls=%fused_computation.37 | convolution fusion | flops 31850496 | bytes 21386240 | tf_op jit(solution)/shard_map/lsij,lsj->li/dot_general | solution.py:134
  216.4 3.4 %fusion.29 = f32[16,1,9,128]{3,1,2,0:T(1,128)S(1)} fusion(bf16[16,144,9,128]{3,1,2,0:T(8,128)(2,1)} %param.23, bf16[16,144,1,1]{1,0,2,3:T(8,128)(2,1)S(1)} %bitcast.109), kind=kOutput, calls=%fused_computation.58 | convolution fusion | flops 5308416 | bytes 5386752 | tf_op jit(solution)/shard_map/lr,lrqp->lqp/dot_general | solution.py:136
  219.8 0.6 copy.91
  (123 shorter events, 9.6 us)
Async XLA Ops:
  0.0 17.7 %copy-start = (bf16[16,144,384]{2,1,0:T(8,128)(2,1)S(1)}, bf16[16,144,384]{2,1,0:T(8,128)(2,1)}, u32[]{:S(2)}) copy-start(bf16[16,144,384]{2,1,0:T(8,128)(2,1)} %param.21) | copy-start | bytes 5308420
  0.9 134.7 %collective-permute-start.1 = (f32[6,2048]{1,0:T(8,128)S(1)}, f32[6,2048]{1,0:T(8,128)S(1)}, u32[]{:S(2)}, u32[]{:S(2)}) collective-permute-start(f32[6,2048]{1,0:T(8,128)S(1)} %get-tuple-element.204), channel_id=1, source_target_pairs={{1,0},{2,1},{3,2},{4,3},{5,4},{6,5},{7,6},{8,7},{9,8},{10,9},{11,1... | collective-permute-start | bytes 147464 | tf_op jit(solution)/shard_map/ppermute | solution.py:20
  3.5 132.1 %collective-permute-start = (f32[6,2048]{1,0:T(8,128)S(1)}, f32[6,2048]{1,0:T(8,128)S(1)}, u32[]{:S(2)}, u32[]{:S(2)}) collective-permute-start(f32[6,2048]{1,0:T(8,128)S(1)} %get-tuple-element.204), channel_id=1, source_target_pairs={{0,1},{1,2},{2,3},{3,4},{4,5},{5,6},{6,7},{7,8},{8,9},{9,10},{10,1... | collective-permute-start | bytes 147464 | tf_op jit(solution)/shard_map/ppermute | solution.py:19
  8.8 117.6 %all-to-all-start = ((s32[32,1,4]{2,1,0:T(1,128)}), s32[32,1,4]{2,1,0:T(1,128)S(1)}, u32[]{:S(2)}, u32[]{:S(2)}) async-start(s32[32,1,4]{2,1,0:T(1,128)} %copy.36), calls=%async_computation | async-start | bytes 32768 | tf_op jit(solution)/shard_map/all_to_all | solution.py:119
  59.0 76.6 %copy-start.2 = (f32[3,2048]{1,0:T(4,128)S(1)}, f32[3,2048]{1,0:T(4,128)}, u32[]{:S(2)}) copy-start(f32[3,2048]{1,0:T(4,128)} %param.14) | copy-start | bytes 73732
  59.0 76.6 %copy-start.3 = (f32[3,2048]{1,0:T(4,128)S(1)}, f32[3,2048]{1,0:T(4,128)}, u32[]{:S(2)}) copy-start(f32[3,2048]{1,0:T(4,128)} %param.13) | copy-start | bytes 73732
  59.0 76.7 %copy-start.4 = (s32[16]{0:T(128)S(1)}, s32[16]{0:T(128)}, u32[]{:S(2)}) copy-start(s32[16]{0:T(128)} %param.16) | copy-start | bytes 196
  129.8 68.2 %all-to-all-start.1 = ((bf16[32,2,288]{2,1,0:T(2,128)(2,1)}), bf16[32,2,288]{2,1,0:T(2,128)(2,1)S(1)}, u32[]{:S(2)}, u32[]{:S(2)}) async-start(bf16[32,2,288]{2,1,0:T(2,128)(2,1)} %reshape.271), calls=%async_computation.1 | async-start | bytes 98304 | tf_op jit(solution)/shard_map/all_to_all | solution.py:121
  192.6 27.2 %collective-permute-start.3 = (f32[16,3,128]{2,0,1:T(8,128)S(1)}, f32[16,3,128]{2,0,1:T(8,128)S(1)}, u32[]{:S(2)}, u32[]{:S(2)}) collective-permute-start(f32[16,3,128]{2,0,1:T(8,128)S(1)} %get-tuple-element.203), channel_id=1, source_target_pairs={{0,1},{1,2},{2,3},{3,4},{4,5},{5,6},{6,7},{7,8},{8,9},{9,10},{10,1... | collective-permute-start | bytes 73736 | tf_op jit(solution)/shard_map/ppermute | solution.py:28
  196.0 23.8 %collective-permute-start.2 = (f32[16,3,128]{2,0,1:T(8,128)S(1)}, f32[16,3,128]{2,0,1:T(8,128)S(1)}, u32[]{:S(2)}, u32[]{:S(2)}) collective-permute-start(f32[16,3,128]{2,0,1:T(8,128)S(1)} %get-tuple-element.202), channel_id=1, source_target_pairs={{1,0},{2,1},{3,2},{4,3},{5,4},{6,5},{7,6},{8,7},{9,8},{10,9},{11,1... | collective-permute-start | bytes 73736 | tf_op jit(solution)/shard_map/ppermute | solution.py:28
  200.6 19.9 %copy-start.1 = (bf16[16,144,384]{2,1,0:T(8,128)(2,1)S(1)}, bf16[16,144,384]{2,1,0:T(8,128)(2,1)}, u32[]{:S(2)}) copy-start(bf16[16,144,384]{2,1,0:T(8,128)(2,1)} %param.21) | copy-start | bytes 5308420
where the time goes:
time: 223 us; the launch traced here: 220 us
  local copies, waits for them, and re-layouts  117 us (52%)
  other arithmetic  55.4 us (25%)
  matrix products  24 us (11%)
  starting transfers between devices  23.3 us (10%)
    gather x2, local copies, waits for them, and re-layouts, per_device(): jnp.take(transfer_table, far_class.reshape(-1), axis=0)  108 us
    reduce_sum x8, other arithmetic, near_step(): src_part = add_rows(src_part, index, -jnp.sum(terms, axis=2))  24.2 us
    reduce_sum x8, other arithmetic, pair_terms(): rho_sq = jnp.sum(sep * sep, axis=1) + BLOB  18 us
    dot_general x1, matrix products, per_device(): jnp.einsum('lsij,lsj->li', operators, sources, preferred_element_type=jnp...  15.7 us
    all_to_all x1, starting transfers between devices, per_device(): lax.all_to_all(replies, 'patch', split_axis=0, concat_axis=0, tiled=True)  5.83 us
    all_to_all x1, starting transfers between devices, per_device(): lax.all_to_all(requests[0], 'patch', split_axis=0, concat_axis=0, tiled=T...  5.73 us
    eq x8, other arithmetic, one_hot(): indices[:, None] == jnp.arange(count, dtype=jnp.int32)[None, :]  5.6 us
    ppermute x2, starting transfers between devices, passed_along(): return lax.ppermute(x, axis, pairs)  5.29 us
  transfers between devices with their start and end apart: 6, of which 0 were waited for; matrix products, arithmetic and copies ran while one was open for 88% of the time, Pallas kernels for 0%

commit v1 on v0

v1 whole, which is shorter than its diff:
```python
import functools
import math

import jax
import jax.numpy as jnp
from jax import lax
from jax.experimental import pallas as pl
from jax.experimental.pallas import tpu as pltpu
from jax.sharding import PartitionSpec as P

KERNEL = 1.0 / (8.0 * math.pi)
BLOB = 0.25
MESH = pl.DeviceIdType.MESH
F32 = jnp.float32
BF16 = jnp.bfloat16


def iota(shape, dim):
    return lax.broadcasted_iota(jnp.int32, shape, dim)


def dot(a, b):
    return jnp.dot(a, b, preferred_element_type=F32)


def exchange(
    n,
    pos,
    dens,
    up_hbm,
    pos_b,
    pos_a,
    dens_b,
    dens_a,
    mom,
    up,
    dens_rows,
    local_sem,
    halo_send,
    halo_recv,
    mom_send,
    mom_recv,
):
    leaves, width = mom.shape[1:]
    size = pos.shape[1] // leaves
    me = lax.axis_index("patch")
    right = lax.rem(me + 1, n)
    left = lax.rem(me + n - 1, n)
    get_up = pltpu.make_async_copy(up_hbm, up, local_sem)
    get_up.start()
    barrier = pltpu.get_barrier_semaphore()

    @pl.loop(1, n)
    def _(k):
        pl.semaphore_signal(
            barrier, inc=1, device_id=(lax.rem(me + k, n),), device_id_type=MESH
        )

    for leaf in range(leaves):
        for c in range(3):
            dens_rows[leaf : leaf + 1, c * size : (c + 1) * size] = dens[
                c : c + 1, leaf * size : (leaf + 1) * size
            ]
    dens_round = dens_rows[...].astype(BF16)
    get_up.wait()
    row = iota((leaves, width), 0)
    total = jnp.zeros((leaves, width), F32)
    for leaf in range(leaves):
        got = lax.dot_general(
            dens_round, up[leaf], (((1,), (1,)), ((), ())), preferred_element_type=F32
        )
        total = total + jnp.where(row == leaf, got, 0.0)
    mom[me] = total.astype(BF16)

    pl.semaphore_wait(barrier, n - 1)
    halos = []
    for k, (src, dst, peer) in enumerate(
        ((pos, pos_b, right), (dens, dens_b, right), (pos, pos_a, left), (dens, dens_a, left))
    ):
        copy = pltpu.make_async_remote_copy(
            src_ref=src,
            dst_ref=dst,
            send_sem=halo_send.at[k],
            recv_sem=halo_recv.at[k],
            device_id=(peer,),
            device_id_type=MESH,
        )
        copy.start()
        halos.append(copy)

    def mom_copy(k):
        return pltpu.make_async_remote_copy(
            src_ref=mom.at[me],
            dst_ref=mom.at[me],
            send_sem=mom_send.at[k],
            recv_sem=mom_recv.at[k],
            device_id=(lax.rem(me + k, n),),
            device_id_type=MESH,
        )

    @pl.loop(1, n)
    def _(k):
        mom_copy(k).start()

    for copy in halos:
        copy.wait_recv()

    @pl.loop(1, n)
    def _(k):
        mom_copy(k).wait_recv()

    for copy in halos:
        copy.wait_send()

    @pl.loop(1, n)
    def _(k):
        mom_copy(k).wait_send()


def near_field(
    near_src,
    near_count,
    first,
    pos,
    dens,
    pos_b,
    pos_a,
    dens_b,
    dens_a,
    near,
    part_b,
    part_a,
    window,
    tb,
    tacc,
    near_t,
    src_acc,
):
    leaves = near_count.shape[0]
    size = pos.shape[1] // leaves
    src_acc[...] = jnp.zeros_like(src_acc)
    window[...] = jnp.zeros_like(window)
    for part, (x, f) in enumerate(((pos_b, dens_b), (pos, dens), (pos_a, dens_a))):
        for leaf in range(leaves):
            lanes = slice(leaf * size, (leaf + 1) * size)
            window[part * leaves + leaf, 0:3, :] = x[:, lanes]
            window[part * leaves + leaf, 3:6, :] = f[:, lanes]

    offset = first[0]
    lane = iota((size, size), 1)

    @pl.loop(0, leaves)
    def _(leaf):
        columns = jnp.transpose(window[leaves + leaf])
        for c in range(6):
            col = columns[:, c : c + 1]
            if c >= 3:
                col = col * KERNEL
            tb[c] = jnp.broadcast_to(col, (size, size))
        tacc[...] = jnp.zeros_like(tacc)

        def near_block(slot, carry):
            index = near_src[slot, leaf] - offset
            other = window[index]
            xs = [jnp.broadcast_to(other[c : c + 1], (8, size)) for c in range(3)]
            fs = [jnp.broadcast_to(other[c : c + 1], (8, size)) for c in range(3, 6)]
            src_sum = [None] * 3
            for g in range(size // 8):
                r8 = slice(g * 8, (g + 1) * 8)
                ft = [tb[3 + c, r8, :] for c in range(3)]
                sep = [tb[c, r8, :] - xs[c] for c in range(3)]
                rho = sep[0] * sep[0] + sep[1] * sep[1] + sep[2] * sep[2] + BLOB
                inv1 = lax.rsqrt(rho)
                inv2 = inv1 * inv1
                inv3 = inv1 * inv2
                ab = ft[0] * fs[0] + ft[1] * fs[1] + ft[2] * fs[2]
                ar = ft[0] * sep[0] + ft[1] * sep[1] + ft[2] * sep[2]
                br = fs[0] * sep[0] + fs[1] * sep[1] + fs[2] * sep[2]
                p = br * inv3
                q = ar * inv3
                w = ab * inv3 + (3.0 * (p * ar)) * inv2
                for c in range(3):
                    t = ft[c] * p + fs[c] * q - w * sep[c]
                    tacc[c, r8, :] += t
                    src_sum[c] = t if g == 0 else src_sum[c] + t
            for c in range(3):
                src_acc[index, c] += src_sum[c]
            return carry

        lax.fori_loop(0, near_count[leaf], near_block, 0)
        cols = [jnp.sum(tacc[c], axis=1, keepdims=True) for c in range(3)]
        mixed = jnp.where(lane == 0, cols[0], jnp.where(lane == 1, cols[1], cols[2]))
        near_t[leaf] = jnp.transpose(mixed)[0:8]

    for part, buf in ((0, part_b), (2, part_a)):
        for leaf in range(leaves):
            for c in range(3):
                buf[c : c + 1, leaf * size : (leaf + 1) * size] = jnp.sum(
                    src_acc[part * leaves + leaf, c], axis=0, keepdims=True
                )
    for leaf in range(leaves):
        for c in range(3):
            near[c : c + 1, leaf * size : (leaf + 1) * size] = near_t[
                leaf, c : c + 1, :
            ] - jnp.sum(src_acc[leaves + leaf, c], axis=0, keepdims=True)


def far_field(
    far_count,
    dens,
    far_slot,
    far_class,
    req,
    mom,
    table_hbm,
    down_hbm,
    far_out,
    table,
    down,
    hot_class,
    hot_slot,
    tiled,
    sums,
    fold,
    expan,
    far_acc,
    table_sem,
    down_sem,
):
    n, leaves, width = mom.shape
    size = dens.shape[1] // leaves
    far_num = far_slot.shape[1]
    classes = table.shape[0]
    cap = req.shape[1]
    block = fold.shape[0]

    def table_copy(b):
        lanes = pl.ds(pl.multiple_of(b * block, 128), block)
        return pltpu.make_async_copy(
            table_hbm.at[:, lanes], table.at[:, lanes], table_sem.at[b]
        )

    for b in range(width * width // block):
        table_copy(b).start()
    get_down = pltpu.make_async_copy(down_hbm, down, down_sem)
    get_down.start()
    count_col = jnp.zeros((leaves, 1), jnp.int32)
    leaf_col = iota((leaves, 1), 0)
    for leaf in range(leaves):
        count_col = jnp.where(leaf_col == leaf, far_count[leaf], count_col)
    class_iota = iota((leaves, classes), 1)
    dev_iota = iota((leaves, n), 1) * cap
    for s in range(far_num):
        rows = slice(s * leaves, (s + 1) * leaves)
        wanted = jnp.where(s < count_col, far_class[:, s : s + 1], -1)
        hot_class[rows, :] = (class_iota == wanted).astype(F32).astype(BF16)
        slot = far_slot[:, s : s + 1]
        for place in range(cap):
            hot_slot[place, rows, :] = (dev_iota + place == slot).astype(F32).astype(BF16)
    fold_row = iota(fold.shape, 0)
    fold_first = iota(fold.shape, 1) * width
    fold[...] = (
        ((fold_row >= fold_first) & (fold_row < fold_first + width)).astype(F32).astype(BF16)
    )
    period = tiled.shape[1]
    spread_gap = iota((width, period), 1) - iota((width, period), 0)
    spread = spread_gap == 0
    for k in range(1, period // width):
        spread = spread | (spread_gap == k * width)
    spread = spread.astype(F32).astype(BF16)
    moments = mom[...].reshape(n * leaves, width)
    leaf_iota = iota((n, n * leaves), 1) - iota((n, n * leaves), 0) * leaves
    picked = []
    for place in range(cap):
        pick = (leaf_iota == req[:, place : place + 1]).astype(F32).astype(BF16)
        chosen = dot(pick, moments).astype(BF16)
        picked.append(dot(chosen, spread).astype(BF16))
    for k in range(period // 128):
        lanes = slice(k * 128, (k + 1) * 128)
        acc = dot(hot_slot[0], picked[0][:, lanes])
        for place in range(1, cap):
            acc = acc + dot(hot_slot[place], picked[place][:, lanes])
        tiled[:, lanes] = acc

    expan[...] = jnp.zeros_like(expan)
    step = 256 if block % 256 == 0 else 128
    per_block = block // width

    @pl.loop(0, width * width // block)
    def _(b):
        table_copy(b).wait()
        for t in range(block // step):
            start = pl.multiple_of(b * block + t * step, 128)
            oper = dot(hot_class[...], table[:, pl.ds(start, step)])
            for h in range(step // 128):
                at = ((t * step) // 128 + h) % (period // 128)
                acc = None
                for s in range(far_num):
                    rows = slice(s * leaves, (s + 1) * leaves)
                    term = oper[rows, h * 128 : (h + 1) * 128] * tiled[
                        rows, at * 128 : (at + 1) * 128
                    ]
                    acc = term if acc is None else acc + term
                sums[:, t * step + h * 128 : t * step + (h + 1) * 128] = acc
        whole = sums[...]
        high = whole.astype(BF16)
        low = (whole - high.astype(F32)).astype(BF16)
        res = dot(high, fold[...]) + dot(low, fold[...])
        wide = jnp.concatenate([res, jnp.zeros((leaves, expan.shape[1] - 128), F32)], axis=1)
        expan[...] += pltpu.roll(wide, b * per_block, 1)

    expansion = expan[...][:, :width].astype(BF16)
    get_down.wait()
    far_acc[...] = jnp.zeros_like(far_acc)
    leaf_row = iota((leaves, size), 0)

    @pl.loop(0, leaves)
    def _(leaf):
        lanes = pl.ds(pl.multiple_of(leaf * size, size), size)
        own = dens[:, lanes]
        fields = [dot(expansion, down[leaf, q]) for q in range(9)]
        for k in range(3):
            far = (
                own[0:1] * fields[k] + own[1:2] * fields[3 + k] + own[2:3] * fields[6 + k]
            )
            far_acc[k] += jnp.where(leaf_row == leaf, far, 0.0)

    for leaf in range(leaves):
        for c in range(3):
            far_out[c : c + 1, leaf * size : (leaf + 1) * size] = far_acc[
                c, leaf : leaf + 1, :
            ]


def per_device(
    n,
    positions,
    densities,
    near_src,
    near_count,
    far_slot,
    far_class,
    far_count,
    requests,
    up_basis,
    transfer_table,
    down_basis,
):
    leaves = near_count.shape[0]
    nodes = positions.shape[1]
    size = nodes // leaves
    width = up_basis.shape[1]
    far_num = far_slot.shape[1]
    cap = requests.shape[2]
    classes = transfer_table.shape[0]
    period = math.lcm(width, 128)
    blocks = width * width // period
    block = 2 * period if blocks % 2 == 0 else period
    down = jnp.transpose(down_basis, (0, 2, 1, 3))
    blocks = width * width // block
    smem = pl.BlockSpec(memory_space=pltpu.SMEM)
    vmem = pl.BlockSpec(memory_space=pltpu.VMEM)
    hbm = pl.BlockSpec(memory_space=pl.ANY)
    line = jax.ShapeDtypeStruct((3, nodes), F32)
    limit = 60 * 1024 * 1024
    pos_b, pos_a, dens_b, dens_a, mom = pl.pallas_call(
        functools.partial(exchange, n),
        out_shape=[line] * 4 + [jax.ShapeDtypeStruct((n, leaves, width), BF16)],
        in_specs=[vmem] * 2 + [hbm],
        out_specs=[vmem] * 5,
        scratch_shapes=[
            pltpu.VMEM(up_basis.shape, BF16),
            pltpu.VMEM((leaves, 3 * size), F32),
            pltpu.SemaphoreType.DMA,
            pltpu.SemaphoreType.DMA((4,)),
            pltpu.SemaphoreType.DMA((4,)),
            pltpu.SemaphoreType.DMA((n,)),
            pltpu.SemaphoreType.DMA((n,)),
        ],
        compiler_params=pltpu.CompilerParams(
            collective_id=0, has_side_effects=True, vmem_limit_bytes=limit
        ),
    )(positions, densities, up_basis)
    first = ((lax.axis_index("patch") - 1) * leaves).reshape(1)
    near, part_b, part_a = pl.pallas_call(
        near_field,
        out_shape=[line] * 3,
        in_specs=[smem] * 3 + [vmem] * 6,
        out_specs=[vmem] * 3,
        scratch_shapes=[
            pltpu.VMEM((3 * leaves, 8, size), F32),
            pltpu.VMEM((6, size, size), F32),
            pltpu.VMEM((3, size, size), F32),
            pltpu.VMEM((leaves, 8, size), F32),
            pltpu.VMEM((3 * leaves, 3, 8, size), F32),
        ],
        compiler_params=pltpu.CompilerParams(vmem_limit_bytes=limit),
    )(near_src.T, near_count, first, positions, densities, pos_b, pos_a, dens_b, dens_a)
    up_pairs = [(i, i + 1) for i in range(n - 1)]
    got_a = lax.ppermute(part_b, "patch", [(j, i) for i, j in up_pairs])
    got_b = lax.ppermute(part_a, "patch", up_pairs)
    far = pl.pallas_call(
        far_field,
        out_shape=line,
        in_specs=[smem] + [vmem] * 5 + [hbm] * 2,
        out_specs=vmem,
        scratch_shapes=[
            pltpu.VMEM(transfer_table.shape, BF16),
            pltpu.VMEM(down.shape, BF16),
            pltpu.VMEM((far_num * leaves, classes), BF16),
            pltpu.VMEM((cap, far_num * leaves, n), BF16),
            pltpu.VMEM((far_num * leaves, period), F32),
            pltpu.VMEM((leaves, block), F32),
            pltpu.VMEM((block, 128), BF16),
            pltpu.VMEM((leaves, (width + 127) // 128 * 128), F32),
            pltpu.VMEM((3, leaves, size), F32),
            pltpu.SemaphoreType.DMA((blocks,)),
            pltpu.SemaphoreType.DMA,
        ],
        cost_estimate=pl.CostEstimate(
            flops=2 * far_num * leaves * 256 * width * width,
            bytes_accessed=2 * (transfer_table.size + down.size),
            transcendentals=0,
        ),
        compiler_params=pltpu.CompilerParams(vmem_limit_bytes=limit),
    )(far_count, densities, far_slot, far_class, requests[0], mom, transfer_table, down)
    return near + far - got_a - got_b


def solution(mesh):
    placed = (
        P(None, "patch"),
        P(None, "patch"),
        P("patch", None),
        P("patch"),
        P("patch", None),
        P("patch", None),
        P("patch"),
        P("patch", None, None),
        P("patch", None, None),
        P(),
        P("patch", None, None, None),
    )
    return jax.shard_map(
        functools.partial(per_device, mesh.shape["patch"]),
        mesh=mesh,
        in_specs=placed,
        out_specs=P(None, "patch"),
        check_vma=False,
    )
```

time: 223 us -> 60.7 us (0.27); the launches traced: 220 us -> 60.6 us
  local copies, waits for them, and re-layouts: 117 us -> 1.36 us
  other arithmetic: 55.4 us -> 1.39 us
  Pallas kernels: 0 us -> 51.4 us
  matrix products: 24 us -> 0 us
  starting transfers between devices: 23.3 us -> 6.45 us
    gather x4 -> x0, local copies, waits for them, and re-layouts: 111 us -> none  [the longest x2 108 us: per_device(): jnp.take(transfer_table, far_class.reshape(-1), axis=0)]
    pallas_call x0 -> x3, Pallas kernels: none -> 51.4 us  [the longest x1 18.5 us: per_device(): pl.pallas_call(near_field, out_shape=[line] * 3, in_specs=[smem] * 3 + [v...]
    reduce_sum x16 -> x0, other arithmetic: 42.2 us -> none  [the longest x8 24.2 us: near_step(): src_part = add_rows(src_part, index, -jnp.sum(terms, axis=2))]
    dot_general x19 -> x0, matrix products: 24 us -> none  [the longest x1 15.7 us: per_device(): jnp.einsum('lsij,lsj->li', operators, sources, preferred_element_type=jnp...]
    all_to_all x2 -> x0, starting transfers between devices: 11.6 us -> none  [the longest x1 5.83 us: per_device(): lax.all_to_all(replies, 'patch', split_axis=0, concat_axis=0, tiled=True)]
    eq x8 -> x0, other arithmetic: 5.6 us -> none  [one_hot(): indices[:, None] == jnp.arange(count, dtype=jnp.int32)[None, :]]
    ppermute x4 -> x2, starting transfers between devices: 11.8 us -> 6.45 us  [the longest x1 4.54 us: per_device(): got_b = lax.ppermute(part_a, 'patch', up_pairs)]
    div x8 -> x0, other arithmetic: 3.44 us -> none  [pair_terms(): inv_three = inv_one / rho_sq]
  transfers between devices with their start and end apart: 6 -> 2, of which waited for: 0 -> 0; matrix products, arithmetic and copies ran while one was open for 88% -> 2% of each run, Pallas kernels for 0% -> 30%
where the time goes in v1:
time: 60.7 us; the launch traced here: 60.6 us
  Pallas kernels  51.4 us (85%)
  starting transfers between devices  6.45 us (11%)
  other arithmetic  1.39 us (2%)
  local copies, waits for them, and re-layouts  1.36 us (2%)
    pallas_call x1, Pallas kernels, per_device(): pl.pallas_call(near_field, out_shape=[line] * 3, in_specs=[smem] * 3 + [v...  18.5 us
    pallas_call x1, Pallas kernels, per_device(): pl.pallas_call(far_field, out_shape=line, in_specs=[smem] + [vmem] * 5 +...  18.2 us
    pallas_call x1, Pallas kernels, per_device(): pl.pallas_call(functools.partial(exchange, n), out_shape=[line] * 4 + [ja...  14.7 us
    ppermute x1, starting transfers between devices, per_device(): got_b = lax.ppermute(part_a, 'patch', up_pairs)  4.54 us
    ppermute x1, starting transfers between devices, per_device(): got_a = lax.ppermute(part_b, 'patch', [(j, i) for i, j in up_pairs])  1.91 us
    sub x1, other arithmetic, per_device(): return near + far - got_a - got_b  1.39 us
    squeeze x1, local copies, waits for them, and re-layouts, per_device(): requests[0]  1.36 us
  transfers between devices with their start and end apart: 2, of which 0 were waited for; matrix products, arithmetic and copies ran while one was open for 2% of the time, Pallas kernels for 30%

profile of v1, /device:TPU:3, one launch (start us, length us, event | category | flops | bytes accessed | tf_op | source)
XLA Modules:
  0.0 60.6 jit_solution(12238549808116576877)
XLA Ops:
  0.0 14.7 %shard_map.109 = (f32[3,2048]{1,0:T(4,128)}, f32[3,2048]{1,0:T(4,128)}, f32[3,2048]{1,0:T(4,128)}, f32[3,2048]{1,0:T(4,128)}, bf16[32,16,144]{2,1,0:T(8,128)(2,1)}) custom-call(f32[3,2048]{1,0:T(4,128)} %pos.3, f32[3,2048]{1,0:T(4,128)} %dens.5, bf16[16,144,384]{2,1,0:T(8,128)(2,1)} %up_hbm.1), custom_call_target="tpu_custom_call" | custom-call | tf_op jit(solution)/shard_map/pallas_call | solution.py:366
  14.7 18.5 %shard_map.110 = (f32[3,2048]{1,0:T(4,128)}, f32[3,2048]{1,0:T(4,128)}, f32[3,2048]{1,0:T(4,128)}) custom-call(s32[8,16]{1,0:T(8,128)} %bitcast.4, s32[16]{0:T(128)} %near_count.1, s32[1]{0:T(128)} %bitcast.1.first, f32[3,2048]{1,0:T(4,128)} %pos.3, f32[3,2048]{1,0:T(4,128)} %dens.5, f32[3,2048]{1,0:T(4,128)} %get-tuple-element.13.pos_b, ...), custom_call_target="tpu_custom_call" | custom-call | tf_op jit(solution)/shard_map/pallas_call | solution.py:385
  33.2 1.9 %collective-permute-start = (f32[3,2048]{1,0:T(4,128)}, f32[3,2048]{1,0:T(4,128)S(1)}, u32[]{:S(2)}, u32[]{:S(2)}) collective-permute-start(f32[3,2048]{1,0:T(4,128)} %get-tuple-element.19), channel_id=1, source_target_pairs={{1,0},{2,1},{3,2},{4,3},{5,4},{6,5},{7,6},{8,7},{9,8},{10,9},{11,1... | collective-permute-start | bytes 73736 | tf_op jit(solution)/shard_map/ppermute | solution.py:400
  35.1 4.5 %collective-permute-start.1 = (f32[3,2048]{1,0:T(4,128)}, f32[3,2048]{1,0:T(4,128)S(1)}, u32[]{:S(2)}, u32[]{:S(2)}) collective-permute-start(f32[3,2048]{1,0:T(4,128)} %get-tuple-element.20), channel_id=1, source_target_pairs={{0,1},{1,2},{2,3},{3,4},{4,5},{5,6},{6,7},{7,8},{8,9},{9,10},{10,1... | collective-permute-start | bytes 73736 | tf_op jit(solution)/shard_map/ppermute | solution.py:401
  39.7 1.4 %copy.12.req = s32[32,4]{1,0:T(8,128)} copy(s32[32,4]{0,1:T(4,128)} %bitcast.5) | data formatting | bytes 1024 | tf_op jit(solution)/shard_map/squeeze | solution.py:426
  41.0 0.0 copy-start
  41.0 18.2 %shard_map.111 = f32[3,2048]{1,0:T(4,128)} custom-call(s32[16]{0:T(128)} %far_count.1, f32[3,2048]{1,0:T(4,128)} %dens.5, s32[16,32]{1,0:T(8,128)} %far_slot.1, s32[16,32]{1,0:T(8,128)} %far_class.1, s32[32,4]{1,0:T(8,128)} %copy.12.req, bf16[32,16,144]{2,1,0:T(8,128)(2,1)} %get-tuple-element.18.mom, bf16[189,20736]{1,0:T(8,128)(2,1)} %table_hbm.1, ...), custom_call_target="tpu_custom_call" | custom-call | flops 5435817984 | bytes 13146624 | tf_op jit(solution)/shard_map/pallas_call | solution.py:402
  59.2 0.0 collective-permute-done
  59.2 0.0 collective-permute-done.1
  59.2 0.0 copy-done
  59.2 1.4 %subtract_subtract_fusion = f32[3,2048]{1,0:T(4,128)} fusion(f32[3,2048]{1,0:T(4,128)S(1)} %collective-permute-done.1, f32[3,2048]{1,0:T(4,128)S(1)} %collective-permute-done, f32[3,2048]{1,0:T(4,128)S(1)} %copy-done, f32[3,2048]{1,0:T(4,128)} %shard_map.111), kind=kLoop, calls=%fused_computation | loop fusion | flops 18432 | bytes 122880 | tf_op jit(solution)/shard_map/sub | solution.py:427
Async XLA Ops:
  33.2 26.0 %collective-permute-start = (f32[3,2048]{1,0:T(4,128)}, f32[3,2048]{1,0:T(4,128)S(1)}, u32[]{:S(2)}, u32[]{:S(2)}) collective-permute-start(f32[3,2048]{1,0:T(4,128)} %get-tuple-element.19), channel_id=1, source_target_pairs={{1,0},{2,1},{3,2},{4,3},{5,4},{6,5},{7,6},{8,7},{9,8},{10,9},{11,1... | collective-permute-start | bytes 73736 | tf_op jit(solution)/shard_map/ppermute | solution.py:400
  35.1 24.1 %collective-permute-start.1 = (f32[3,2048]{1,0:T(4,128)}, f32[3,2048]{1,0:T(4,128)S(1)}, u32[]{:S(2)}, u32[]{:S(2)}) collective-permute-start(f32[3,2048]{1,0:T(4,128)} %get-tuple-element.20), channel_id=1, source_target_pairs={{0,1},{1,2},{2,3},{3,4},{4,5},{5,6},{6,7},{7,8},{8,9},{9,10},{10,1... | collective-permute-start | bytes 73736 | tf_op jit(solution)/shard_map/ppermute | solution.py:401
  41.0 18.2 %copy-start = (f32[3,2048]{1,0:T(4,128)S(1)}, f32[3,2048]{1,0:T(4,128)}, u32[]{:S(2)}) copy-start(f32[3,2048]{1,0:T(4,128)} %get-tuple-element.17) | copy-start | bytes 73732

commit v2 on v1

--- a/solution.py
+++ b/solution.py
@@ -38,10 +38,8 @@
     local_sem,
     halo_send,
     halo_recv,
-    mom_send,
-    mom_recv,
 ):
-    leaves, width = mom.shape[1:]
+    leaves, width = mom.shape
     size = pos.shape[1] // leaves
     me = lax.axis_index("patch")
     right = lax.rem(me + 1, n)
@@ -50,11 +48,8 @@
     get_up.start()
     barrier = pltpu.get_barrier_semaphore()
 
-    @pl.loop(1, n)
-    def _(k):
-        pl.semaphore_signal(
-            barrier, inc=1, device_id=(lax.rem(me + k, n),), device_id_type=MESH
-        )
+    for peer in (left, right):
+        pl.semaphore_signal(barrier, inc=1, device_id=(peer,), device_id_type=MESH)
 
     for leaf in range(leaves):
         for c in range(3):
@@ -62,17 +57,7 @@
                 c : c + 1, leaf * size : (leaf + 1) * size
             ]
     dens_round = dens_rows[...].astype(BF16)
-    get_up.wait()
-    row = iota((leaves, width), 0)
-    total = jnp.zeros((leaves, width), F32)
-    for leaf in range(leaves):
-        got = lax.dot_general(
-            dens_round, up[leaf], (((1,), (1,)), ((), ())), preferred_element_type=F32
-        )
-        total = total + jnp.where(row == leaf, got, 0.0)
-    mom[me] = total.astype(BF16)
-
-    pl.semaphore_wait(barrier, n - 1)
+    pl.semaphore_wait(barrier, 2)
     halos = []
     for k, (src, dst, peer) in enumerate(
         ((pos, pos_b, right), (dens, dens_b, right), (pos, pos_a, left), (dens, dens_a, left))
@@ -88,33 +73,18 @@
         copy.start()
         halos.append(copy)
 
-    def mom_copy(k):
-        return pltpu.make_async_remote_copy(
-            src_ref=mom.at[me],
-            dst_ref=mom.at[me],
-            send_sem=mom_send.at[k],
-            recv_sem=mom_recv.at[k],
-            device_id=(lax.rem(me + k, n),),
-            device_id_type=MESH,
-        )
-
-    @pl.loop(1, n)
-    def _(k):
-        mom_copy(k).start()
+    get_up.wait()
+    row = iota((leaves, width), 0)
+    total = jnp.zeros((leaves, width), F32)
+    for leaf in range(leaves):
+        got = lax.dot_general(
+            dens_round, up[leaf], (((1,), (1,)), ((), ())), preferred_element_type=F32
+        )
+        total = total + jnp.where(row == leaf, got, 0.0)
+    mom[...] = total.astype(BF16)
 
     for copy in halos:
-        copy.wait_recv()
-
-    @pl.loop(1, n)
-    def _(k):
-        mom_copy(k).wait_recv()
-
-    for copy in halos:
-        copy.wait_send()
-
-    @pl.loop(1, n)
-    def _(k):
-        mom_copy(k).wait_send()
+        copy.wait()
 
 
 def near_field(
@@ -206,15 +176,22 @@
 
 
 def far_field(
+    n,
     far_count,
     dens,
     far_slot,
     far_class,
     req,
-    mom,
+    mom_own,
+    near,
+    part_b,
+    part_a,
     table_hbm,
     down_hbm,
-    far_out,
+    out,
+    mom,
+    got_b,
+    got_a,
     table,
     down,
     hot_class,
@@ -226,12 +203,25 @@
     far_acc,
     table_sem,
     down_sem,
+    mom_send,
+    mom_recv,
+    part_send,
+    part_recv,
 ):
-    n, leaves, width = mom.shape
+    leaves, width = mom_own.shape
+    me = lax.axis_index("patch")
+    barrier = pltpu.get_barrier_semaphore()
+
+    @pl.loop(1, n)
+    def _(k):
+        pl.semaphore_signal(
+            barrier, inc=1, device_id=(lax.rem(me + k, n),), device_id_type=MESH
+        )
+
     size = dens.shape[1] // leaves
     far_num = far_slot.shape[1]
     classes = table.shape[0]
-    cap = req.shape[1]
+    cap = req.shape[0]
     block = fold.shape[0]
 
     def table_copy(b):
@@ -249,31 +239,75 @@
     for leaf in range(leaves):
         count_col = jnp.where(leaf_col == leaf, far_count[leaf], count_col)
     class_iota = iota((leaves, classes), 1)
-    dev_iota = iota((leaves, n), 1) * cap
     for s in range(far_num):
         rows = slice(s * leaves, (s + 1) * leaves)
         wanted = jnp.where(s < count_col, far_class[:, s : s + 1], -1)
         hot_class[rows, :] = (class_iota == wanted).astype(F32).astype(BF16)
-        slot = far_slot[:, s : s + 1]
-        for place in range(cap):
-            hot_slot[place, rows, :] = (dev_iota + place == slot).astype(F32).astype(BF16)
     fold_row = iota(fold.shape, 0)
     fold_first = iota(fold.shape, 1) * width
     fold[...] = (
         ((fold_row >= fold_first) & (fold_row < fold_first + width)).astype(F32).astype(BF16)
     )
+    pl.semaphore_wait(barrier, n - 1)
+
+    def mom_copy(k):
+        return pltpu.make_async_remote_copy(
+            src_ref=mom_own,
+            dst_ref=mom.at[me],
+            send_sem=mom_send.at[k],
+            recv_sem=mom_recv.at[k],
+            device_id=(lax.rem(me + k, n),),
+            device_id_type=MESH,
+        )
+
+    @pl.loop(1, n)
+    def _(k):
+        mom_copy(k).start()
+
+    parts = []
+    for k, (src, dst, peer) in enumerate(
+        (
+            (part_b, got_a, lax.rem(me + n - 1, n)),
+            (part_a, got_b, lax.rem(me + 1, n)),
+        )
+    ):
+        copy = pltpu.make_async_remote_copy(
+            src_ref=src,
+            dst_ref=dst,
+            send_sem=part_send.at[k],
+            recv_sem=part_recv.at[k],
+            device_id=(peer,),
+            device_id_type=MESH,
+        )
+        copy.start()
+        parts.append(copy)
+
+    mom[me] = mom_own[...]
+    dev_iota = iota((leaves, n), 1) * cap
+    for s in range(far_num):
+        rows = slice(s * leaves, (s + 1) * leaves)
+        slot = far_slot[:, s : s + 1]
+        for place in range(cap):
+            hot_slot[place, rows, :] = (dev_iota + place == slot).astype(F32).astype(BF16)
     period = tiled.shape[1]
     spread_gap = iota((width, period), 1) - iota((width, period), 0)
     spread = spread_gap == 0
     for k in range(1, period // width):
         spread = spread | (spread_gap == k * width)
     spread = spread.astype(F32).astype(BF16)
+
+    @pl.loop(1, n)
+    def _(k):
+        mom_copy(k).wait_recv()
+
     moments = mom[...].reshape(n * leaves, width)
-    leaf_iota = iota((n, n * leaves), 1) - iota((n, n * leaves), 0) * leaves
+    leaf_iota = iota((n * leaves, n), 0) - iota((n * leaves, n), 1) * leaves
     picked = []
     for place in range(cap):
-        pick = (leaf_iota == req[:, place : place + 1]).astype(F32).astype(BF16)
-        chosen = dot(pick, moments).astype(BF16)
+        pick = (leaf_iota == req[place : place + 1, :]).astype(F32).astype(BF16)
+        chosen = lax.dot_general(
+            pick, moments, (((0,), (0,)), ((), ())), preferred_element_type=F32
+        ).astype(BF16)
         picked.append(dot(chosen, spread).astype(BF16))
     for k in range(period // 128):
         lanes = slice(k * 128, (k + 1) * 128)
@@ -325,11 +359,19 @@
             )
             far_acc[k] += jnp.where(leaf_row == leaf, far, 0.0)
 
+    for copy in parts:
+        copy.wait_recv()
     for leaf in range(leaves):
+        lanes = slice(leaf * size, (leaf + 1) * size)
         for c in range(3):
-            far_out[c : c + 1, leaf * size : (leaf + 1) * size] = far_acc[
-                c, leaf : leaf + 1, :
-            ]
+            came = got_b[c : c + 1, lanes] + got_a[c : c + 1, lanes]
+            out[c : c + 1, lanes] = near[c : c + 1, lanes] - came + far_acc[c, leaf : leaf + 1, :]
+    for copy in parts:
+        copy.wait_send()
+
+    @pl.loop(1, n)
+    def _(k):
+        mom_copy(k).wait_send()
 
 
 def per_device(
@@ -365,7 +407,7 @@
     limit = 60 * 1024 * 1024
     pos_b, pos_a, dens_b, dens_a, mom = pl.pallas_call(
         functools.partial(exchange, n),
-        out_shape=[line] * 4 + [jax.ShapeDtypeStruct((n, leaves, width), BF16)],
+        out_shape=[line] * 4 + [jax.ShapeDtypeStruct((leaves, width), BF16)],
         in_specs=[vmem] * 2 + [hbm],
         out_specs=[vmem] * 5,
         scratch_shapes=[
@@ -374,8 +416,6 @@
             pltpu.SemaphoreType.DMA,
             pltpu.SemaphoreType.DMA((4,)),
             pltpu.SemaphoreType.DMA((4,)),
-            pltpu.SemaphoreType.DMA((n,)),
-            pltpu.SemaphoreType.DMA((n,)),
         ],
         compiler_params=pltpu.CompilerParams(
             collective_id=0, has_side_effects=True, vmem_limit_bytes=limit
@@ -396,15 +436,15 @@
         ],
         compiler_params=pltpu.CompilerParams(vmem_limit_bytes=limit),
     )(near_src.T, near_count, first, positions, densities, pos_b, pos_a, dens_b, dens_a)
-    up_pairs = [(i, i + 1) for i in range(n - 1)]
-    got_a = lax.ppermute(part_b, "patch", [(j, i) for i, j in up_pairs])
-    got_b = lax.ppermute(part_a, "patch", up_pairs)
-    far = pl.pallas_call(
-        far_field,
+    return pl.pallas_call(
+        functools.partial(far_field, n),
         out_shape=line,
-        in_specs=[smem] + [vmem] * 5 + [hbm] * 2,
+        in_specs=[smem] + [vmem] * 8 + [hbm] * 2,
         out_specs=vmem,
         scratch_shapes=[
+            pltpu.VMEM((n, leaves, width), BF16),
+            pltpu.VMEM((3, nodes), F32),
+            pltpu.VMEM((3, nodes), F32),
             pltpu.VMEM(transfer_table.shape, BF16),
             pltpu.VMEM(down.shape, BF16),
             pltpu.VMEM((far_num * leaves, classes), BF16),
@@ -416,15 +456,27 @@
             pltpu.VMEM((3, leaves, size), F32),
             pltpu.SemaphoreType.DMA((blocks,)),
             pltpu.SemaphoreType.DMA,
+            pltpu.SemaphoreType.DMA((n,)),
+            pltpu.SemaphoreType.DMA((n,)),
+            pltpu.SemaphoreType.DMA((2,)),
+            pltpu.SemaphoreType.DMA((2,)),
         ],
-        cost_estimate=pl.CostEstimate(
-            flops=2 * far_num * leaves * 256 * width * width,
-            bytes_accessed=2 * (transfer_table.size + down.size),
-            transcendentals=0,
+        compiler_params=pltpu.CompilerParams(
+            collective_id=1, has_side_effects=True, vmem_limit_bytes=limit
         ),
-        compiler_params=pltpu.CompilerParams(vmem_limit_bytes=limit),
-    )(far_count, densities, far_slot, far_class, requests[0], mom, transfer_table, down)
-    return near + far - got_a - got_b
+    )(
+        far_count,
+        densities,
+        far_slot,
+        far_class,
+        requests[0].T,
+        mom,
+        near,
+        part_b,
+        part_a,
+        transfer_table,
+        down,
+    )
 
 
 def solution(mesh):

time: 60.7 us -> 58 us (0.956)
  starting transfers between devices: 6.45 us -> 0 us
  Pallas kernels: 51.4 us -> 56.2 us
  other arithmetic: 1.39 us -> 0 us
    pallas_call x1, Pallas kernels: 18.2 us -> 37.6 us  [per_device(): pl.pallas_call(functools.partial(far_field, n), out_shape=line, in_specs=...]
    pallas_call x1, Pallas kernels: 14.7 us -> 6.76 us  [per_device(): pl.pallas_call(functools.partial(exchange, n), out_shape=[line] * 4 + [ja...]
    pallas_call x1, Pallas kernels: 18.5 us -> 11.9 us  [per_device(): pl.pallas_call(near_field, out_shape=[line] * 3, in_specs=[smem] * 3 + [v...]
    ppermute x2 -> x0, starting transfers between devices: 6.45 us -> none  [the longest x1 4.54 us: per_device(): got_b = lax.ppermute(part_a, 'patch', up_pairs)]
    sub x1 -> x0, other arithmetic: 1.39 us -> none  [per_device(): return near + far - got_a - got_b]
    unnamed x2 -> x1, local copies, waits for them, and re-layouts: 0.01 us -> 1.38 us
    squeeze x1 -> x0, local copies, waits for them, and re-layouts: 1.36 us -> none  [per_device(): requests[0]]
  transfers between devices with their start and end apart: 2 -> 0, of which waited for: 0 -> 0; matrix products, arithmetic and copies ran while one was open for 2% -> 0% of each run, Pallas kernels for 30% -> 0%
where the time goes in v2:
time: 58 us; the launch traced here: 57.6 us
  Pallas kernels  56.2 us (97%)
  local copies, waits for them, and re-layouts  1.38 us (2%)
    pallas_call x1, Pallas kernels, per_device(): pl.pallas_call(functools.partial(far_field, n), out_shape=line, in_specs=...  37.6 us
    pallas_call x1, Pallas kernels, per_device(): pl.pallas_call(near_field, out_shape=[line] * 3, in_specs=[smem] * 3 + [v...  11.9 us
    pallas_call x1, Pallas kernels, per_device(): pl.pallas_call(functools.partial(exchange, n), out_shape=[line] * 4 + [ja...  6.76 us
    unnamed x1, local copies, waits for them, and re-layouts  1.38 us

profile of v2, /device:TPU:3, one launch (start us, length us, event | category | flops | bytes accessed | tf_op | source)
XLA Modules:
  0.0 57.6 jit_solution(5879073320507710704)
XLA Ops:
  0.0 6.8 %shard_map.109 = (f32[3,2048]{1,0:T(4,128)}, f32[3,2048]{1,0:T(4,128)}, f32[3,2048]{1,0:T(4,128)}, f32[3,2048]{1,0:T(4,128)}, bf16[16,144]{1,0:T(8,128)(2,1)}) custom-call(f32[3,2048]{1,0:T(4,128)} %pos.3, f32[3,2048]{1,0:T(4,128)} %dens.5, bf16[16,144,384]{2,1,0:T(8,128)(2,1)} %up_hbm.1), custom_call_target="tpu_custom_call" | custom-call | tf_op jit(solution)/shard_map/pallas_call | solution.py:408
  6.8 11.9 %shard_map.110 = (f32[3,2048]{1,0:T(4,128)}, f32[3,2048]{1,0:T(4,128)}, f32[3,2048]{1,0:T(4,128)}) custom-call(s32[8,16]{1,0:T(8,128)} %bitcast.7, s32[16]{0:T(128)} %near_count.1, s32[1]{0:T(128)} %bitcast.3.first, f32[3,2048]{1,0:T(4,128)} %pos.3, f32[3,2048]{1,0:T(4,128)} %dens.5, f32[3,2048]{1,0:T(4,128)} %get-tuple-element.14.pos_b, ...), custom_call_target="tpu_custom_call" | custom-call | tf_op jit(solution)/shard_map/pallas_call | solution.py:425
  18.6 37.6 %shard_map.111 = f32[3,2048]{1,0:T(4,128)} custom-call(s32[16]{0:T(128)} %far_count.1, f32[3,2048]{1,0:T(4,128)} %dens.5, s32[16,32]{1,0:T(8,128)} %far_slot.1, s32[16,32]{1,0:T(8,128)} %far_class.1, s32[4,32]{1,0:T(4,128)} %bitcast.8, bf16[16,144]{1,0:T(8,128)(2,1)} %get-tuple-element.13.mom_own, f32[3,2048]{1,0:T(4,128)} %get-tuple-element.18.near, ...), custom_call_target="tpu_custom_call" | custom-call | tf_op jit(solution)/shard_map/pallas_call | solution.py:439
  56.2 1.4 %copy.13 = f32[3,2048]{1,0:T(4,128)} copy(f32[3,2048]{1,0:T(4,128)} %shard_map.111) | data formatting | bytes 49152
